TPU v7x, 32 devices: a whole 2x2x4 slice. The times are simulated.
32 devices in a mesh: batch: 4 (over z), seq: 4 (over y, core), head: 2 (over x).
Axes of the slice: x: 2, y: 2, z: 4, core: 2. Of those that a mesh axis runs over, the one named last changes fastest.
Arguments:
- image_hidden: bfloat16 [8, 1024, 3072], P('batch', 'seq', 'head'), parts along dimension 0, may hold values from -6 to 6
- modulation: float32 [8, 3, 3072], P('batch'), parts along dimension 0, may hold values from -4 to 4
- qkv_weight: bfloat16 [3072, 3, 1536], P(None, None, 'head'), may hold values from -0.109375 to 0.109375
- out_weight: bfloat16 [1536, 3072], P('head'), may hold values from -0.15625 to 0.15625
- q_gain: float32 [128], replicated, may hold values from 1.2 to 2.5
- k_gain: float32 [128], replicated, may hold values from 1.2 to 2.5
- text_keys: bfloat16 [8, 128, 1536], P('batch', 'seq', 'head'), parts along dimension 0, may hold values from -10 to 10
- text_values: bfloat16 [8, 128, 1536], P('batch', 'seq', 'head'), parts along dimension 0, may hold values from -6 to 6
- stale_keys: bfloat16 [8, 1024, 1536], P('batch', 'seq', 'head'), parts along dimension 0, may hold values from -64 to 64
- stale_values: bfloat16 [8, 1024, 1536], P('batch', 'seq', 'head'), parts along dimension 0, may hold values from -6 to 6
- cached_residual: bfloat16 [8, 1024, 3072], P('batch', 'seq', 'head'), parts along dimension 0, may hold values from -6 to 6
- patch_of: int32 [16], P('batch'), parts along dimension 0, may hold values from 0 to 3, each once
- refresh: int32 [16], P('batch'), parts along dimension 0, may hold values from 0 to 1, as said below
- text_len: int32 [8], P('batch'), parts along dimension 0, may hold values from 16 to 128
Outputs:
- image_out: bfloat16 [8, 1024, 3072], P('batch', 'seq', 'head'), parts along dimension 0
There are 4 independent parts, one for each index of `batch`. A program takes and returns all parts, laid end to end along the dimension named above; an argument that names none is the same for every part. Nothing has to cross between parts.
Inputs may be any that keep to these rules, and one draw needn't show every extreme that they name: `patch_of`: A permutation: every image band sits on exactly one index of seq. `refresh`: exactly 1 entries are 1, the rest 0.
All inputs are finite; a program needn't handle non-finite values.
Results may differ from a plain program's by a relative error of at most 0.012.
The roundings to bfloat16 on the way count: a program that leaves them out, or rounds other values in their place, can miss the bound.
Values may be sent and summed in bfloat16 or wider, within the bound.
A program may use at most 192 MiB of HBM per device.

v0:
```python
import jax
import jax.numpy as jnp
from jax import lax
from jax.sharding import PartitionSpec as P

GRID_W = 64


epsilon = 1e-06


def rotary_tables(raster, head_dim, grid_width):
    half_dim = head_dim // 2
    first_pairs = head_dim // 16
    axis_pairs = (half_dim - first_pairs) // 2
    pair_index = jnp.arange(half_dim, dtype=jnp.int32)
    pair_local = jnp.where(
        pair_index < first_pairs + axis_pairs,
        pair_index - first_pairs,
        pair_index - first_pairs - axis_pairs,
    )
    exponent = -pair_local.astype(jnp.float32) / float(axis_pairs)
    frequency = jnp.where(
        pair_index < first_pairs, jnp.float32(0.0), jnp.power(jnp.float32(10000.0), exponent)
    )
    row_pos = (raster // grid_width).astype(jnp.float32)
    col_pos = (raster % grid_width).astype(jnp.float32)
    position = jnp.where(
        pair_index[None, :] < first_pairs + axis_pairs, row_pos[:, None], col_pos[:, None]
    )
    angles = position * frequency[None, :]
    cosine = jnp.cos(angles)
    sine = jnp.sin(angles)
    return (jnp.concatenate([cosine, cosine], axis=-1), jnp.concatenate([-sine, sine], axis=-1))


def rms_rotate(vectors, gain_vec, cos_full, sin_full):
    scaled = (
        vectors
        * lax.rsqrt(jnp.mean(vectors * vectors, axis=-1, keepdims=True) + epsilon)
        * gain_vec
    )
    half_dim = vectors.shape[-1] // 2
    return (
        scaled * cos_full[None, :, None, :]
        + jnp.roll(scaled, half_dim, axis=-1) * sin_full[None, :, None, :]
    )


def per_device(
    image_hidden,
    modulation,
    qkv_weight,
    out_weight,
    q_gain,
    k_gain,
    text_keys,
    text_values,
    stale_keys,
    stale_values,
    cached_residual,
    patch_of,
    refresh,
    text_len,
):
    prompts, tok_rows, width_part = image_hidden.shape
    head_dim = q_gain.shape[0]
    channels = out_weight.shape[0]
    local_heads = channels // head_dim
    seq_seat = lax.axis_index("seq")
    head_seat = lax.axis_index("head")
    gathered = lax.all_gather(image_hidden, "head", axis=2, tiled=True)
    model_width = gathered.shape[2]
    hidden_f32 = gathered.astype(jnp.float32)
    row_mean = jnp.mean(hidden_f32, axis=-1, keepdims=True)
    centered = hidden_f32 - row_mean
    variance = jnp.mean(centered * centered, axis=-1, keepdims=True)
    normed = centered * lax.rsqrt(variance + epsilon)
    modulated = (
        normed * (1.0 + modulation[:, 1][:, None, :]) + modulation[:, 0][:, None, :]
    ).astype(jnp.bfloat16)
    projected = jnp.dot(
        modulated.reshape(prompts * tok_rows, model_width),
        qkv_weight.reshape(model_width, 3 * channels),
        preferred_element_type=jnp.float32,
    )
    projected = projected.reshape(prompts, tok_rows, 3, local_heads, head_dim)
    seat_ids = jnp.arange(patch_of.shape[0], dtype=jnp.int32)
    own_band = jnp.sum(jnp.where(seat_ids == seq_seat, patch_of, 0))
    own_flag = jnp.sum(jnp.where(seat_ids == seq_seat, refresh, 0))
    raster = own_band * tok_rows + jnp.arange(tok_rows, dtype=jnp.int32)
    cos_full, sin_full = rotary_tables(raster, head_dim, GRID_W)
    fresh_q = rms_rotate(projected[:, :, 0], q_gain, cos_full, sin_full).astype(jnp.bfloat16)
    fresh_k = rms_rotate(projected[:, :, 1], k_gain, cos_full, sin_full).astype(jnp.bfloat16)
    fresh_v = projected[:, :, 2].astype(jnp.bfloat16)
    fresh_k_flat = fresh_k.reshape(prompts, tok_rows, channels)
    fresh_v_flat = fresh_v.reshape(prompts, tok_rows, channels)
    score_scale = head_dim ** (-0.5)
    text_k, text_v = (
        lax.all_gather(text_keys, "seq", axis=1, tiled=True),
        lax.all_gather(text_values, "seq", axis=1, tiled=True),
    )
    total_text = text_k.shape[1]
    text_key_rows = text_k.reshape(prompts, total_text, local_heads, head_dim)
    text_value_rows = text_v.reshape(prompts, total_text, local_heads, head_dim)
    text_scores = (
        jnp.einsum("pqhd,pkhd->phqk", fresh_q, text_key_rows, preferred_element_type=jnp.float32)
        * score_scale
    )
    text_valid = jnp.arange(total_text, dtype=jnp.int32)[None, :] < text_len[:, None]
    text_scores = jnp.where(text_valid[:, None, None, :], text_scores, -1e30)
    row_top = jnp.max(text_scores, axis=-1)
    text_weights = jnp.exp(text_scores - row_top[..., None])
    row_total = jnp.sum(text_weights, axis=-1)
    weighted = jnp.einsum(
        "phqk,pkhd->phqd",
        text_weights.astype(jnp.bfloat16),
        text_value_rows,
        preferred_element_type=jnp.float32,
    )
    running = (row_top, row_total, weighted)
    chosen_k = jnp.where(own_flag == 1, fresh_k_flat, stale_keys)
    chosen_v = jnp.where(own_flag == 1, fresh_v_flat, stale_values)
    key_rows = lax.all_gather(chosen_k[None], "seq", axis=0, tiled=True)
    value_rows = lax.all_gather(chosen_v[None], "seq", axis=0, tiled=True)
    piece_count = key_rows.shape[0]
    is_mine = jnp.arange(piece_count, dtype=jnp.int32) == seq_seat
    key_rows = jnp.where(is_mine[:, None, None, None], fresh_k_flat[None], key_rows)
    value_rows = jnp.where(is_mine[:, None, None, None], fresh_v_flat[None], value_rows)
    key_rows = key_rows.reshape(piece_count, prompts, tok_rows, local_heads, head_dim)
    value_rows = value_rows.reshape(piece_count, prompts, tok_rows, local_heads, head_dim)
    old_top, old_total, old_weighted = running
    scores = (
        jnp.einsum("pqhd,npkhd->phqnk", fresh_q, key_rows, preferred_element_type=jnp.float32)
        * score_scale
    )
    new_top = jnp.maximum(old_top, jnp.max(scores, axis=(3, 4)))
    shrink = jnp.exp(old_top - new_top)
    weights = jnp.exp(scores - new_top[..., None, None])
    new_total = old_total * shrink + jnp.sum(weights, axis=(3, 4))
    added = jnp.einsum(
        "phqnk,npkhd->phqd",
        weights.astype(jnp.bfloat16),
        value_rows,
        preferred_element_type=jnp.float32,
    )
    running = (new_top, new_total, old_weighted * shrink[..., None] + added)
    final_top, final_total, final_weighted = running
    attended = (final_weighted / final_total[..., None]).astype(jnp.bfloat16)
    partial_value = jnp.einsum(
        "phqd,hde->pqe",
        attended,
        out_weight.reshape(local_heads, head_dim, model_width),
        preferred_element_type=jnp.float32,
    )
    reduced = lax.psum_scatter(
        partial_value.astype(jnp.bfloat16), "head", scatter_dimension=2, tiled=True
    ).astype(jnp.float32)
    gate_part = lax.dynamic_slice_in_dim(modulation[:, 2], head_seat * width_part, width_part, 1)
    result = (
        image_hidden.astype(jnp.float32)
        + gate_part[:, None, :] * reduced
        + cached_residual.astype(jnp.float32)
    )
    return result.astype(jnp.bfloat16)


def solution(mesh):
    in_specs = (
        P("batch", "seq", "head"),
        P("batch", None, None),
        P(None, None, "head"),
        P("head", None),
        P(),
        P(),
        P("batch", "seq", "head"),
        P("batch", "seq", "head"),
        P("batch", "seq", "head"),
        P("batch", "seq", "head"),
        P("batch", "seq", "head"),
        P("batch"),
        P("batch"),
        P("batch"),
    )
    out_specs = P("batch", "seq", "head")
    return jax.shard_map(
        per_device, mesh=mesh, in_specs=in_specs, out_specs=out_specs, check_vma=False
    )
```

profile of v0, /device:TPU:0, one launch (start us, length us, event | category | flops | bytes accessed | tf_op | source)
XLA Modules:
  0.0 229.6 jit_solution(13103266877624958867)
XLA Ops:
  6.5 0.7 all-gather.6.cloned.1.call-update
  7.3 18.8 %copy.40 = bf16[3072,3,768]{0,2,1:T(8,128)(2,1)} copy(bf16[3072,3,768]{2,0,1:T(8,128)(2,1)} %param.16) | data formatting | bytes 28311552 | tf_op args[2]
  26.1 0.7 select_reduce_fusion
  27.5 0.3 fusion.45
  27.9 0.6 copy-done.9
  28.6 1.2 copy.52
  29.8 0.7 copy-done.11
  30.5 1.2 copy.51
  32.4 0.6 fusion.59
  33.0 23.5 %all-gather.6.cloned.1.call-done = bf16[2,256,3072]{2,1,0:T(8,128)(2,1)} async-done(((bf16[2,256,1536]{2,1,0:T(8,128)(2,1)}), bf16[2,256,3072]{2,1,0:T(8,128)(2,1)}) %all-gather.6.cloned.1.call-update) | async-done | bytes 3145744 | tf_op jit(solution)/shard_map/all_gather | solution.py:72
  56.5 2.5 %convert_reduce_fusion = f32[2,256]{1,0:T(2,128)S(1)} fusion(bf16[2,256,3072]{2,1,0:T(8,128)(2,1)} %all-gather.6.cloned.1.call-done), kind=kLoop, calls=%fused_computation.5 | loop fusion | flops 3145216 | bytes 3147776 | tf_op jit(solution)/shard_map/reduce_sum | solution.py:75
  59.1 0.3 copy-done.2
  59.4 1.0 fusion.4
  60.3 10.8 %fusion.13 = f32[2,256,3,6,128]{1,4,3,2,0:T(8,128)S(1)} fusion(bf16[3,6,128,3072,1]{3,2,1,0,4:T(8,128)(2,1)} %bitcast.73, bf16[2,256,3072]{2,1,0:T(8,128)(2,1)S(1)} %copy-done.2, f32[2,3072]{1,0:T(2,128)S(1)} %get-tuple-element.18, f32[2,3072]{1,0:T(2,128)S(1)} %get-tuple-element.19, f32[2,256]{1,0:T(2,128)S(1)} %add_rsqrt_fusion.2, ...), kind=kOutput, calls=%fused_computation.17 | convolution fusion | flops 7257194496 | bytes 22073344 | tf_op jit(solution)/shard_map/dot_general | solution.py:82
  71.2 0.3 fusion.26
  71.5 1.8 copy-done.1
  73.3 0.4 fusion.27
  73.7 0.2 fusion.57
  74.0 1.6 copy.53
  75.6 1.3 mul.206
  76.8 3.1 %copy.50 = f32[2,256,768]{2,1,0:T(8,128)} copy(f32[2,256,768]{1,2,0:T(8,128)} %bitcast.80) | data formatting | bytes 3145728 | tf_op jit(solution)/shard_map/mul | solution.py:39
  79.9 1.6 copy.49
  81.5 4.8 %broadcast_select_fusion.3 = (bf16[2,256,768]{2,1,0:T(8,128)(2,1)}, bf16[2,256,768]{2,1,0:T(8,128)(2,1)}) fusion(bf16[2,256,768]{2,1,0:T(8,128)(2,1)} %param.22, pred[]{:T(512)S(6)} %eq.22, f32[2,256,768]{2,1,0:T(8,128)} %copy.53, f32[256,768]{1,0:T(8,128)} %copy.52, f32[256,768]{1,0:T(8,128)} %copy.51, f32[768]{0:T(1024)S(1)} %broadcast_bitcast_fusion, ...), kind=kLoop, calls=%fused_computation.54 | loop fusion | flops 2752512 | bytes 8653825 | tf_op jit(solution)/shard_map/jit(_where)/select_n | solution.py:122
  86.4 1.5 slice.60
  87.9 0.3 copy.58
  88.2 2.1 broadcast_select_fusion.2
  90.5 7.0 %all_gather.16 = bf16[2,128,768]{2,0,1:T(2,128)(2,1)} all-gather(bf16[2,32,768]{2,0,1:T(2,128)(2,1)S(1)} %copy.41), channel_id=1, replica_groups=mesh['batch'=4,'seq'=4,'head'=2] {'seq'}, dimensions={1}, use_global_device_ids=true | all-gather | bytes 491520 | tf_op jit(solution)/shard_map/all_gather | solution.py:100
  97.5 1.3 copy.42
  98.8 1.0 copy.45
  99.9 10.2 %all_gather.17 = bf16[2,128,768]{2,0,1:T(2,128)(2,1)} all-gather(bf16[2,32,768]{2,0,1:T(2,128)(2,1)S(1)} %copy.45), channel_id=1, replica_groups=mesh['batch'=4,'seq'=4,'head'=2] {'seq'}, dimensions={1}, use_global_device_ids=true | all-gather | bytes 491520 | tf_op jit(solution)/shard_map/all_gather | solution.py:101
  110.1 1.3 copy.46
  111.5 0.6 iota_compare_fusion.1
  112.1 1.2 copy.54
  113.5 0.4 fusion.23
  113.9 0.9 copy-done.3
  114.7 0.4 fusion.60
  115.2 0.2 fusion.36
  115.4 1.6 fusion.38
  117.1 3.2 %copy.55 = bf16[8,256,768]{1,2,0:T(8,128)(2,1)S(1)} copy(bf16[8,256,768]{2,1,0:T(8,128)(2,1)} %all-gather.8.cloned.1.call-done) | data formatting | bytes 6291456 | tf_op jit(solution)/shard_map/all_gather | solution.py:124
  120.3 26.9 %all-gather.10.cloned.1.call-done = bf16[8,256,768]{2,1,0:T(8,128)(2,1)} async-done(((bf16[2,256,768]{2,1,0:T(8,128)(2,1)}), bf16[8,256,768]{2,1,0:T(8,128)(2,1)}) %all-gather.10.cloned.1.call-update) | async-done | bytes 3145744 | tf_op jit(solution)/shard_map/all_gather | solution.py:125
  147.2 4.7 %copy.59 = bf16[8,256,768]{1,2,0:T(8,128)(2,1)} copy(bf16[8,256,768]{2,1,0:T(8,128)(2,1)} %all-gather.10.cloned.1.call-done) | data formatting | bytes 6291456 | tf_op jit(solution)/shard_map/all_gather | solution.py:125
  151.9 4.6 %broadcast_select_fusion.1 = (bf16[4,2,256,768]{2,3,1,0:T(8,128)(2,1)S(1)}, bf16[4,2,256,768]{2,3,1,0:T(8,128)(2,1)}) fusion(bf16[4,2,256,768]{2,3,1,0:T(8,128)(2,1)S(1)} %bitcast.75, pred[4]{0:T(512)(128)(4,1)S(1)} %copy-done.17, bf16[2,256,768]{1,2,0:T(8,128)(2,1)} %copy.54, bf16[4,2,256,768]{2,3,1,0:T(8,128)(2,1)} %bitcast.76, ...), kind=kLoop, calls=%fused_computation.27 | loop fusion | flops 3145728 | bytes 14155780 | tf_op jit(solution)/shard_map/jit(_where)/select_n | solution.py:128
  156.5 3.0 %multiply_reduce_fusion = (f32[2,6,256]{2,1,0:T(8,128)S(1)}, f32[2,6,256,4,256]{2,4,3,1,0:T(8,128)S(1)}) fusion(bf16[4,2,256,6,128]{2,4,3,1,0:T(8,128)(2,1)S(1)} %bitcast.74, bf16[2,256,6,128]{1,3,2,0:T(8,128)(2,1)} %copy-done.3), kind=kOutput, calls=%fused_computation.1 | convolution fusion | flops 811594752 | bytes 16527360 | tf_op jit(solution)/shard_map/pqhd,npkhd->phqnk/dot_general | solution.py:134
  159.5 2.1 fusion
  161.7 3.1 %copy-done = f32[2,6,256,4,256]{2,4,3,1,0:T(8,128)} copy-done((f32[2,6,256,4,256]{2,4,3,1,0:T(8,128)}, f32[2,6,256,4,256]{2,4,3,1,0:T(8,128)S(1)}, u32[]{:S(2)}) %copy-start) | copy-done | bytes 12582936
  164.9 11.3 %bitcast_convert_fusion = bf16[2,256,3072]{2,1,0:T(8,128)(2,1)} fusion(bf16[6,128,3072,1]{2,1,0,3:T(8,128)(2,1)} %bitcast.86, f32[2,6,256,128]{3,2,1,0:T(8,128)} %fusion.38, bf16[4,2,256,6,128]{2,4,3,1,0:T(8,128)(2,1)S(1)} %bitcast.83, f32[2,6,256,4,256]{2,4,3,1,0:T(8,128)} %copy-done, f32[2,6,256]{2,1,0:T(8,128)S(1)} %max.14, ...), kind=kOutput, calls=%fused_computation.13 | convolution fusion | flops 3233808384 | bytes 25202688 | tf_op jit(solution)/shard_map/phqd,hde->pqe/dot_general | solution.py:150
  176.3 43.6 %reduce-scatter.2.cloned.1.call-done = bf16[2,256,1536]{2,1,0:T(8,128)(2,1)} async-done(((bf16[2,256,3072]{2,1,0:T(8,128)(2,1)}), bf16[2,256,1536]{2,1,0:T(8,128)(2,1)}) %reduce-scatter.2.cloned.1.call-update) | async-done | bytes 1572880 | tf_op jit(solution)/shard_map/reduce_scatter | solution.py:156
  219.8 3.2 %add_convert_fusion = bf16[2,256,1536]{2,1,0:T(8,128)(2,1)} fusion(bf16[2,256,1536]{2,1,0:T(8,128)(2,1)S(1)} %copy-done.8, bf16[2,256,1536]{2,1,0:T(8,128)(2,1)} %reduce-scatter.2.cloned.1.call-done, bf16[2,256,1536]{2,1,0:T(8,128)(2,1)S(1)} %copy-done.5, f32[2,1536]{1,0:T(2,128)S(1)} %dynamic-slice_bitcast_fusion), kind=kLoop, calls=%fused_computation.21 | loop fusion | flops 5505024 | bytes 6303744 | tf_op jit(solution)/shard_map/convert_element_type | solution.py:165
  (67 shorter events, 1.0 us)
Async XLA Ops:
  6.5 50.0 %all-gather.6.cloned.1.call-start = ((), (), s32[]{:S(2)}) async-start(), calls=%async_computation.1 | async-start | bytes 4718592 | tf_op jit(solution)/shard_map/all_gather | solution.py:72
  7.3 109.8 %all-gather.8.cloned.1.call-start = ((), (), s32[]{:S(2)}) async-start(), calls=%async_computation.3 | async-start | bytes 3932160 | tf_op jit(solution)/shard_map/all_gather | solution.py:124
  7.3 18.8 %copy-start.18 = (s32[4]{0:T(128)S(1)}, s32[4]{0:T(128)}, u32[]{:S(2)}) copy-start(s32[4]{0:T(128)} %param.26) | copy-start | bytes 52
  7.3 18.8 %copy-start.19 = (s32[4]{0:T(128)S(1)}, s32[4]{0:T(128)}, u32[]{:S(2)}) copy-start(s32[4]{0:T(128)} %param.25) | copy-start | bytes 52
  26.1 6.2 %copy-start.16 = (f32[128]{0:T(128)S(1)}, f32[128]{0:T(128)}, u32[]{:S(2)}) copy-start(f32[128]{0:T(128)} %param.19) | copy-start | bytes 1540
  26.1 6.2 %copy-start.14 = (f32[2,3,3072]{2,0,1:T(2,128)S(1)}, f32[2,3,3072]{2,0,1:T(2,128)}, u32[]{:S(2)}) copy-start(f32[2,3,3072]{2,0,1:T(2,128)} %param.15) | copy-start | bytes 221188
  27.9 0.7 copy-start.9
  29.8 0.7 copy-start.11
  56.5 2.8 %copy-start.2 = (bf16[2,256,3072]{2,1,0:T(8,128)(2,1)S(1)}, bf16[2,256,3072]{2,1,0:T(8,128)(2,1)}, u32[]{:S(2)}) copy-start(bf16[2,256,3072]{2,1,0:T(8,128)(2,1)} %all-gather.6.cloned.1.call-done) | copy-start | bytes 9437188
  71.2 2.1 copy-start.1
  71.2 2.1 copy-start.20
  75.6 4.3 %slice-start = ((f32[2,256,3,6,128]{1,4,3,2,0:T(8,128)}), f32[2,256,1,6,128]{1,4,3,2,0:T(8,128)S(1)}, s32[]{:S(2)}) async-start(f32[2,256,3,6,128]{1,4,3,2,0:T(8,128)} %copy-done.1), calls=%async_computation.5 | async-start | bytes 3145728 | tf_op jit(solution)/shard_map/slice | solution.py:94
  86.3 4.1 %copy-start.13 = (bf16[2,32,768]{2,1,0:T(8,128)(2,1)S(1)}, bf16[2,32,768]{2,1,0:T(8,128)(2,1)}, u32[]{:S(2)}) copy-start(bf16[2,32,768]{2,1,0:T(8,128)(2,1)} %param.20) | copy-start | bytes 294916
  86.3 60.9 %all-gather.10.cloned.1.call-start = ((), (), s32[]{:S(2)}) async-start(), calls=%async_computation.4 | async-start | bytes 3932160 | tf_op jit(solution)/shard_map/all_gather | solution.py:125
  87.9 12.0 %copy-start.4 = (bf16[2,256,1,6,128]{1,4,3,2,0:T(8,128)(2,1)}, bf16[2,256,1,6,128]{1,4,3,2,0:T(8,128)(2,1)S(1)}, u32[]{:S(2)}) copy-start(bf16[2,256,1,6,128]{1,4,3,2,0:T(8,128)(2,1)S(1)} %slice.60) | copy-start | bytes 2359300
  88.2 23.9 %copy-start.21 = (s32[2]{0:T(128)S(1)}, s32[2]{0:T(128)}, u32[]{:S(2)}) copy-start(s32[2]{0:T(128)} %param.27) | copy-start | bytes 28
  90.3 21.8 %copy-start.7 = (bf16[2,256,768]{2,1,0:T(8,128)(2,1)S(1)}, bf16[2,256,768]{2,1,0:T(8,128)(2,1)}, u32[]{:S(2)}) copy-start(bf16[2,256,768]{2,1,0:T(8,128)(2,1)} %get-tuple-element.10) | copy-start | bytes 2359300
  90.3 129.5 %reduce-scatter.2.cloned.1.call-start = ((), (), s32[]{:S(2)}) async-start(), calls=%async_computation.2 | async-start | bytes 4718592 | tf_op jit(solution)/shard_map/reduce_scatter | solution.py:156
  110.1 3.3 %copy-start.10 = (f32[256,128]{0,1:T(8,128)S(1)}, f32[256,128]{0,1:T(8,128)}, u32[]{:S(2)}) copy-start(f32[256,128]{0,1:T(8,128)} %copy-done.9) | copy-start | bytes 393220
  110.1 3.4 %copy-start.12 = (f32[256,128]{0,1:T(8,128)S(1)}, f32[256,128]{0,1:T(8,128)}, u32[]{:S(2)}) copy-start(f32[256,128]{0,1:T(8,128)} %copy-done.11) | copy-start | bytes 393220
  113.9 0.9 copy-start.3
  120.3 31.6 %copy-start.17 = (pred[4]{0:T(512)(128)(4,1)S(1)}, pred[4]{0:T(512)(128)(4,1)}, u32[]{:S(2)}) copy-start(pred[4]{0:T(512)(128)(4,1)} %iota_compare_fusion.1) | copy-start | bytes 16
  159.5 5.3 %copy-start = (f32[2,6,256,4,256]{2,4,3,1,0:T(8,128)}, f32[2,6,256,4,256]{2,4,3,1,0:T(8,128)S(1)}, u32[]{:S(2)}) copy-start(f32[2,6,256,4,256]{2,4,3,1,0:T(8,128)S(1)} %get-tuple-element.28) | copy-start | bytes 37748740
  159.5 5.3 %copy-start.6 = (bf16[4,2,256,768]{2,3,1,0:T(8,128)(2,1)S(1)}, bf16[4,2,256,768]{2,3,1,0:T(8,128)(2,1)}, u32[]{:S(2)}) copy-start(bf16[4,2,256,768]{2,3,1,0:T(8,128)(2,1)} %get-tuple-element.24) | copy-start | bytes 9437188
  164.9 11.4 %copy-start.15 = (f32[2,1,3072]{2,0,1:T(2,128)S(1)}, f32[2,1,3072]{2,0,1:T(2,128)}, u32[]{:S(2)}) copy-start(f32[2,1,3072]{2,0,1:T(2,128)} %get-tuple-element.17) | copy-start | bytes 73732
  176.2 43.6 %copy-start.5 = (bf16[2,256,1536]{2,1,0:T(8,128)(2,1)S(1)}, bf16[2,256,1536]{2,1,0:T(8,128)(2,1)}, u32[]{:S(2)}) copy-start(bf16[2,256,1536]{2,1,0:T(8,128)(2,1)} %param.14) | copy-start | bytes 4718596
  176.2 43.6 %copy-start.8 = (bf16[2,256,1536]{2,1,0:T(8,128)(2,1)S(1)}, bf16[2,256,1536]{2,1,0:T(8,128)(2,1)}, u32[]{:S(2)}) copy-start(bf16[2,256,1536]{2,1,0:T(8,128)(2,1)} %param.24) | copy-start | bytes 4718596
Sparse Core Ops, SparseCore 0:
  8.9 47.6 all-gather.5
  86.4 30.6 all-gather.7
  118.7 28.4 all-gather.9
  176.4 43.4 reduce-scatter.1
where the time goes:
time: 231 us; the launch traced here: 230 us
  waiting for transfers between devices  94.8 us (41%)
  local copies, waits for them, and re-layouts  51.2 us (22%)
  matrix products  27.2 us (12%)
  other arithmetic  24.2 us (10%)
  blocking collectives  17.3 us (7%)
  between operations  14.8 us (6%)
    reduce_scatter x1, waiting for transfers between devices, per_device(): lax.psum_scatter(partial_value.astype(jnp.bfloat16), 'head', scatter_dime...  43.6 us
    unnamed x47, local copies, waits for them, and re-layouts  27.4 us
    all_gather x1, waiting for transfers between devices, per_device(): value_rows = lax.all_gather(chosen_v[None], 'seq', axis=0, tiled=True)  26.9 us
    all_gather x1, waiting for transfers between devices, per_device(): gathered = lax.all_gather(image_hidden, 'head', axis=2, tiled=True)  23.5 us
    dot_general x1, matrix products, per_device(): jnp.einsum('phqd,hde->pqe', attended, out_weight.reshape(local_heads, hea...  11.3 us
    dot_general x1, matrix products, per_device(): jnp.dot(modulated.reshape(prompts * tok_rows, model_width), qkv_weight.re...  10.8 us
    all_gather x1, blocking collectives, per_device(): lax.all_gather(text_values, 'seq', axis=1, tiled=True)  10.2 us
    all_gather x1, blocking collectives, per_device(): lax.all_gather(text_keys, 'seq', axis=1, tiled=True)  7.02 us
  transfers between devices with their start and end apart: 4, of which 4 were waited for; matrix products, arithmetic and copies ran while one was open for 17% of the time, Pallas kernels for 0%

commit v1 on v0

v1 whole, which is shorter than its diff:
```python
import functools

import jax
import jax.numpy as jnp
from jax import lax
from jax.experimental import pallas as pl
from jax.experimental.pallas import tpu as pltpu
from jax.sharding import PartitionSpec as P

GRID_W = 64
CHUNKS = 2
TILE = 512
PAIR = 256

epsilon = 1e-06
LOG2E = 1.4426950408889634


def rotary_tables(raster, head_dim, grid_width):
    half_dim = head_dim // 2
    first_pairs = head_dim // 16
    axis_pairs = (half_dim - first_pairs) // 2
    pair_index = jnp.arange(half_dim, dtype=jnp.int32)
    pair_local = jnp.where(
        pair_index < first_pairs + axis_pairs,
        pair_index - first_pairs,
        pair_index - first_pairs - axis_pairs,
    )
    exponent = -pair_local.astype(jnp.float32) / float(axis_pairs)
    frequency = jnp.where(
        pair_index < first_pairs, jnp.float32(0.0), jnp.power(jnp.float32(10000.0), exponent)
    )
    row_pos = (raster // grid_width).astype(jnp.float32)
    col_pos = (raster % grid_width).astype(jnp.float32)
    position = jnp.where(
        pair_index[None, :] < first_pairs + axis_pairs, row_pos[:, None], col_pos[:, None]
    )
    angles = position * frequency[None, :]
    cosine = jnp.cos(angles)
    sine = jnp.sin(angles)
    return (jnp.concatenate([cosine, cosine], axis=-1), jnp.concatenate([-sine, sine], axis=-1))


def rms_rotate(vectors, gain, cos_rows, sin_rows):
    mean_square = jnp.mean(vectors * vectors, axis=-1, keepdims=True)
    scaled = vectors * lax.rsqrt(mean_square + epsilon) * gain
    return scaled * cos_rows + pltpu.roll(scaled, vectors.shape[-1] // 2, 1) * sin_rows


def step_kernel(
    n_seq,
    refresh_ref,
    len_ref,
    mod_ref,
    gq_ref,
    gk_ref,
    cos_ref,
    sin_ref,
    image_ref,
    wqkv_ref,
    wout_ref,
    tk_ref,
    tv_ref,
    sk_ref,
    sv_ref,
    cached_ref,
    out_ref,
    xin,
    weights,
    wout,
    kv,
    chosen,
    queries,
    attended,
    out_send,
    out_recv,
    result,
    text,
    scores,
    modulated,
    load_sem,
    store_sem,
    img_send,
    img_recv,
    text_send,
    text_recv,
    kv_send,
    kv_recv,
    relay_send,
    part_send,
    part_recv,
):
    prompts, tok_rows, width_part = image_ref.shape
    model_width = 2 * width_part
    channels = wout.shape[0]
    head_dim = cos_ref.shape[1]
    heads = channels // head_dim
    text_rows = tk_ref.shape[1]
    total_text = text_rows * n_seq
    rows = tok_rows // CHUNKS
    n_chunks = prompts * CHUNKS
    n_tiles = width_part // TILE
    n_chips = n_seq // 2
    me = lax.axis_index("seq")
    side = lax.axis_index("head")
    core = lax.rem(me, 2)
    chip = me // 2
    other = 1 - side
    sibling = chip * 2 + (1 - core)

    def remote(src, dst, send, recv, where):
        return pltpu.make_async_remote_copy(
            src_ref=src,
            dst_ref=dst,
            send_sem=send,
            recv_sem=recv,
            device_id=where,
            device_id_type=pl.DeviceIdType.MESH,
        )

    loads = [
        pltpu.make_async_copy(image_ref, xin.at[side], load_sem.at[0]),
        pltpu.make_async_copy(wqkv_ref.at[0], weights.at[0], load_sem.at[1]),
        pltpu.make_async_copy(wqkv_ref.at[1], weights.at[1], load_sem.at[2]),
        pltpu.make_async_copy(wqkv_ref.at[2], weights.at[2], load_sem.at[3]),
        pltpu.make_async_copy(sk_ref, chosen.at[0], load_sem.at[4]),
        pltpu.make_async_copy(sv_ref, chosen.at[1], load_sem.at[5]),
        pltpu.make_async_copy(tk_ref, text.at[0, :, pl.ds(me * text_rows, text_rows)], load_sem.at[6]),
        pltpu.make_async_copy(tv_ref, text.at[1, :, pl.ds(me * text_rows, text_rows)], load_sem.at[7]),
        pltpu.make_async_copy(wout_ref, wout, load_sem.at[8]),
        pltpu.make_async_copy(cached_ref, result, load_sem.at[9]),
    ]
    for copy in loads:
        copy.start()

    barrier = pltpu.get_barrier_semaphore()
    for d in range(1, n_seq):
        peer = lax.rem(me + d, n_seq)
        pl.semaphore_signal(barrier, inc=1, device_id={"seq": peer}, device_id_type=pl.DeviceIdType.MESH)
    pl.semaphore_signal(barrier, inc=1, device_id={"head": other}, device_id_type=pl.DeviceIdType.MESH)
    pl.semaphore_wait(barrier, n_seq)

    def image_copy(c, half):
        p, r0 = c // CHUNKS, (c % CHUNKS) * rows
        return remote(
            image_ref.at[p, pl.ds(r0, rows)],
            xin.at[half, p, pl.ds(r0, rows)],
            img_send.at[c],
            img_recv.at[c],
            {"head": other},
        )

    def text_copy(i, owner, d, where):
        return remote(
            (tk_ref, tv_ref)[i],
            text.at[i, :, pl.ds(owner * text_rows, text_rows)],
            text_send.at[i, d],
            text_recv.at[i, owner],
            where,
        )

    def kv_copy(c, src, owner, send, where):
        p, r0 = c // CHUNKS, (c % CHUNKS) * rows
        return remote(
            src.at[:, p, pl.ds(r0, rows)],
            kv.at[owner, :, p, pl.ds(r0, rows)],
            send,
            kv_recv.at[owner, c],
            where,
        )

    def part_copy(p, t):
        return remote(
            out_send.at[p, t],
            out_recv.at[p, t],
            part_send.at[p, t],
            part_recv.at[p, t],
            {"head": other},
        )

    image_copy(0, side).start()
    image_copy(1, side).start()
    for d in range(1, n_seq):
        for i in range(2):
            text_copy(i, me, d, {"seq": lax.rem(me + d, n_seq)}).start()

    fresh_flag = refresh_ref[me] == 1

    def project(c):
        p, r0 = c // CHUNKS, (c % CHUNKS) * rows
        block = pl.ds(r0, rows)
        if c == 0:
            loads[0].wait()
        image_copy(c, other).wait_recv()
        image_copy(c, side).wait_send()
        if c + 2 < n_chunks:
            image_copy(c + 2, side).start()
        left = xin[0, p, block].astype(jnp.float32)
        right = xin[1, p, block].astype(jnp.float32)
        mean = (
            jnp.sum(left, axis=-1, keepdims=True) + jnp.sum(right, axis=-1, keepdims=True)
        ) / model_width
        left = left - mean
        right = right - mean
        variance = (
            jnp.sum(left * left, axis=-1, keepdims=True)
            + jnp.sum(right * right, axis=-1, keepdims=True)
        ) / model_width
        inverse = lax.rsqrt(variance + epsilon)
        for half, values in ((0, left), (1, right)):
            cols = pl.ds(half * width_part, width_part)
            modulated[:, cols] = (
                values * inverse * (1.0 + mod_ref[1, pl.ds(p, 1), cols])
                + mod_ref[0, pl.ds(p, 1), cols]
            ).astype(jnp.bfloat16)
        if c == 0:
            for copy in loads[1:6]:
                copy.wait()
        cos_rows, sin_rows = cos_ref[block, :], sin_ref[block, :]
        gain_q, gain_k = gq_ref[...], gk_ref[...]

        def pair(j, carry):
            start = pl.multiple_of(j * PAIR, PAIR)
            cols = pl.ds(start, PAIR)
            x = modulated[...]

            def rotated(index, gain):
                raw = jnp.dot(x, weights[index, :, cols], preferred_element_type=jnp.float32)
                pieces = [
                    rms_rotate(raw[:, i : i + head_dim], gain, cos_rows, sin_rows)
                    for i in range(0, PAIR, head_dim)
                ]
                return jnp.concatenate(pieces, axis=-1).astype(jnp.bfloat16)

            fresh_k = rotated(1, gain_k)
            kv[me, 0, p, block, cols] = fresh_k
            chosen[0, p, block, cols] = jnp.where(fresh_flag, fresh_k, chosen[0, p, block, cols])
            fresh_v = jnp.dot(x, weights[2, :, cols], preferred_element_type=jnp.float32).astype(
                jnp.bfloat16
            )
            kv[me, 1, p, block, cols] = fresh_v
            chosen[1, p, block, cols] = jnp.where(fresh_flag, fresh_v, chosen[1, p, block, cols])
            queries[p, block, cols] = rotated(0, gain_q)
            return carry

        lax.fori_loop(0, channels // PAIR, pair, 0)
        for d in range(1, n_chips):
            peer = lax.rem(chip + d, n_chips) * 2 + core
            kv_copy(c, chosen, me, kv_send.at[d, c], {"seq": peer}).start()
        kv_copy(c, chosen, me, kv_send.at[0, c], {"seq": sibling}).start()

    def relay(c):
        for d in range(1, n_chips):
            owner = lax.rem(chip + n_chips - d, n_chips) * 2 + core
            kv_copy(c, kv.at[owner], owner, relay_send.at[d, c], {"seq": sibling}).wait_recv()
            kv_copy(c, kv.at[owner], owner, relay_send.at[d, c], {"seq": sibling}).start()

    def arrive(c):
        for d in range(n_chips):
            owner = lax.rem(chip + n_chips - d, n_chips) * 2 + (1 - core)
            kv_copy(c, kv.at[owner], owner, relay_send.at[d, c], {"seq": sibling}).wait_recv()

    def looped(count, body, init):
        if count <= 4:
            for n in range(count):
                init = body(n, init)
            return init
        return lax.fori_loop(0, count, body, init)

    def times_transposed(a, b):
        return lax.dot_general(a, b, (((1,), (1,)), ((), ())), preferred_element_type=jnp.float32)

    factor = head_dim ** (-0.5) * LOG2E

    def attend(p):
        valid = lax.broadcasted_iota(jnp.int32, (1, total_text), 1) < len_ref[p]

        def folded(op, total, values):
            for i in range(0, values.shape[1], 128):
                total = op(total, values[:, i : i + 128])
            return total

        def one_head(h, carry):
            cols = pl.ds(pl.multiple_of(h * head_dim, head_dim), head_dim)
            q = queries[p, :, cols]
            s_text = times_transposed(q, text[0, p, :, cols])
            s_text = jnp.where(valid, s_text, -1e30)
            top = folded(jnp.maximum, jnp.full((tok_rows, 128), -1e30, jnp.float32), s_text)

            def score(n, best):
                s = times_transposed(q, kv[n, 0, p, :, cols])
                scores[n] = s
                return folded(jnp.maximum, best, s)

            top = looped(n_seq, score, top)
            top = jnp.max(top, axis=-1, keepdims=True)
            w_text = jnp.exp2((s_text - top) * factor)
            total = folded(jnp.add, jnp.zeros((tok_rows, 128), jnp.float32), w_text)
            mixed = jnp.dot(
                w_text.astype(jnp.bfloat16), text[1, p, :, cols], preferred_element_type=jnp.float32
            )

            def mix(n, state):
                total, mixed = state
                w = jnp.exp2((scores[n] - top) * factor)
                mixed = mixed + jnp.dot(
                    w.astype(jnp.bfloat16), kv[n, 1, p, :, cols], preferred_element_type=jnp.float32
                )
                return folded(jnp.add, total, w), mixed

            total, mixed = looped(n_seq, mix, (total, mixed))
            total = jnp.sum(total, axis=-1, keepdims=True)
            attended[p, :, cols] = (mixed / total).astype(jnp.bfloat16)
            return carry

        lax.fori_loop(0, heads, one_head, 0)

    def send_parts(p):
        for t in range(n_tiles):
            cols = pl.ds(pl.multiple_of(other * width_part + t * TILE, TILE), TILE)
            out_send[p, t] = jnp.dot(
                attended[p], wout[:, cols], preferred_element_type=jnp.float32
            ).astype(jnp.bfloat16)
            part_copy(p, t).start()

    def store(p, t):
        here = pl.ds(t * TILE, TILE)
        return pltpu.make_async_copy(
            result.at[p, :, here], out_ref.at[p, :, here], store_sem.at[p, t]
        )

    def finish(p):
        for t in range(n_tiles):
            cols = pl.ds(pl.multiple_of(side * width_part + t * TILE, TILE), TILE)
            here = pl.ds(t * TILE, TILE)
            own = jnp.dot(attended[p], wout[:, cols], preferred_element_type=jnp.float32)
            part_copy(p, t).wait_recv()
            gate = mod_ref[2, pl.ds(p, 1), cols]
            result[p, :, here] = (
                xin[side, p, :, here].astype(jnp.float32)
                + gate * (own + out_recv[p, t].astype(jnp.float32))
                + result[p, :, here].astype(jnp.float32)
            ).astype(jnp.bfloat16)
            store(p, t).start()

    project(0)
    for c in range(1, n_chunks):
        project(c)
        relay(c - 1)
        if c == CHUNKS:
            for copy in loads[6:]:
                copy.wait()
            for d in range(1, n_seq):
                for i in range(2):
                    text_copy(i, lax.rem(me + d, n_seq), d, {"seq": sibling}).wait_recv()
        if c >= CHUNKS and c % CHUNKS == 0:
            p = c // CHUNKS - 1
            for k in range(p * CHUNKS, (p + 1) * CHUNKS):
                arrive(k)
            attend(p)
            send_parts(p)
    relay(n_chunks - 1)
    for k in range(n_chunks - CHUNKS, n_chunks):
        arrive(k)
    attend(prompts - 1)
    send_parts(prompts - 1)
    for p in range(prompts):
        finish(p)

    for p in range(prompts):
        for t in range(n_tiles):
            part_copy(p, t).wait_send()
            store(p, t).wait()
    for c in range(n_chunks):
        for d in range(n_chips):
            kv_copy(c, chosen, me, kv_send.at[d, c], {"seq": sibling}).wait_send()
        for d in range(1, n_chips):
            kv_copy(c, chosen, me, relay_send.at[d, c], {"seq": sibling}).wait_send()
    for d in range(1, n_seq):
        for i in range(2):
            text_copy(i, me, d, {"seq": sibling}).wait_send()


def per_device(
    n_seq,
    image_hidden,
    modulation,
    qkv_weight,
    out_weight,
    q_gain,
    k_gain,
    text_keys,
    text_values,
    stale_keys,
    stale_values,
    cached_residual,
    patch_of,
    refresh,
    text_len,
):
    prompts, tok_rows, width_part = image_hidden.shape
    head_dim = q_gain.shape[0]
    channels, model_width = out_weight.shape
    text_rows = text_keys.shape[1]
    seq_seat = lax.axis_index("seq")
    own_band = lax.dynamic_index_in_dim(patch_of, seq_seat, 0, keepdims=False)
    raster = own_band * tok_rows + jnp.arange(tok_rows, dtype=jnp.int32)
    cos_full, sin_full = rotary_tables(raster, head_dim, GRID_W)
    n_chunks = prompts * CHUNKS
    n_tiles = width_part // TILE
    n_chips = n_seq // 2
    bf16 = jnp.bfloat16
    dma = pltpu.SemaphoreType.DMA
    smem = pl.BlockSpec(memory_space=pltpu.SMEM)
    vmem = pl.BlockSpec(memory_space=pltpu.VMEM)
    anywhere = pl.BlockSpec(memory_space=pl.ANY)
    return pl.pallas_call(
        functools.partial(step_kernel, n_seq),
        out_shape=jax.ShapeDtypeStruct(image_hidden.shape, bf16),
        in_specs=[smem] * 2 + [vmem] * 5 + [anywhere] * 8,
        out_specs=anywhere,
        scratch_shapes=[
            pltpu.VMEM((2, prompts, tok_rows, width_part), bf16),
            pltpu.VMEM((3, model_width, channels), bf16),
            pltpu.VMEM((channels, model_width), bf16),
            pltpu.VMEM((n_seq, 2, prompts, tok_rows, channels), bf16),
            pltpu.VMEM((2, prompts, tok_rows, channels), bf16),
            pltpu.VMEM((prompts, tok_rows, channels), bf16),
            pltpu.VMEM((prompts, tok_rows, channels), bf16),
            pltpu.VMEM((prompts, n_tiles, tok_rows, TILE), bf16),
            pltpu.VMEM((prompts, n_tiles, tok_rows, TILE), bf16),
            pltpu.VMEM((prompts, tok_rows, width_part), bf16),
            pltpu.VMEM((2, prompts, text_rows * n_seq, channels), bf16),
            pltpu.VMEM((n_seq, tok_rows, tok_rows), jnp.float32),
            pltpu.VMEM((tok_rows // CHUNKS, model_width), bf16),
            dma((10,)),
            dma((prompts, n_tiles)),
            dma((n_chunks,)),
            dma((n_chunks,)),
            dma((2, n_seq)),
            dma((2, n_seq)),
            dma((n_chips, n_chunks)),
            dma((n_seq, n_chunks)),
            dma((n_chips, n_chunks)),
            dma((prompts, n_tiles)),
            dma((prompts, n_tiles)),
        ],
        compiler_params=pltpu.CompilerParams(
            collective_id=0, has_side_effects=True, vmem_limit_bytes=67043328
        ),
        name="joint_step",
    )(
        refresh,
        text_len,
        jnp.transpose(modulation, (1, 0, 2)),
        q_gain[None],
        k_gain[None],
        cos_full,
        sin_full,
        image_hidden,
        jnp.transpose(qkv_weight, (1, 0, 2)),
        out_weight,
        text_keys,
        text_values,
        stale_keys,
        stale_values,
        cached_residual,
    )


def solution(mesh):
    in_specs = (
        P("batch", "seq", "head"),
        P("batch", None, None),
        P(None, None, "head"),
        P("head", None),
        P(),
        P(),
        P("batch", "seq", "head"),
        P("batch", "seq", "head"),
        P("batch", "seq", "head"),
        P("batch", "seq", "head"),
        P("batch", "seq", "head"),
        P("batch"),
        P("batch"),
        P("batch"),
    )
    out_specs = P("batch", "seq", "head")
    return jax.shard_map(
        functools.partial(per_device, mesh.shape["seq"]),
        mesh=mesh,
        in_specs=in_specs,
        out_specs=out_specs,
        check_vma=False,
    )
```

time: 231 us -> 89.6 us (0.39)
  waiting for transfers between devices: 94.8 us -> 0 us
  Pallas kernels: 0 us -> 82.8 us
  local copies, waits for them, and re-layouts: 51.2 us -> 3.89 us
  matrix products: 27.2 us -> 0 us
  other arithmetic: 24.2 us -> 2.09 us
  blocking collectives: 17.3 us -> 0 us
  between operations: 14.8 us -> 0.68 us
    pallas_call x0 -> x1, Pallas kernels: none -> 82.8 us  [per_device(): pl.pallas_call(functools.partial(step_kernel, n_seq), out_shape=jax.Shape...]
    all_gather x3 -> x0, waiting for transfers between devices: 50.5 us -> none  [the longest x1 26.9 us: per_device(): value_rows = lax.all_gather(chosen_v[None], 'seq', axis=0, tiled=True)]
    reduce_scatter x1 -> x0, waiting for transfers between devices: 43.6 us -> none  [per_device(): lax.psum_scatter(partial_value.astype(jnp.bfloat16), 'head', scatter_dime...]
    dot_general x5 -> x0, matrix products: 27.2 us -> none  [the longest x1 11.3 us: per_device(): jnp.einsum('phqd,hde->pqe', attended, out_weight.reshape(local_heads, hea...]
    unnamed x47 -> x1, local copies, waits for them, and re-layouts: 27.4 us -> 2.65 us
    all_gather x2 -> x0, blocking collectives: 17.3 us -> none  [the longest x1 10.2 us: per_device(): lax.all_gather(text_values, 'seq', axis=1, tiled=True)]
    select_n x3 -> x0, other arithmetic: 11.5 us -> none  [the longest x1 4.75 us: per_device(): chosen_k = jnp.where(own_flag == 1, fresh_k_flat, stale_keys)]
    all_gather x4 -> x0, local copies, waits for them, and re-layouts: 10.5 us -> none  [the longest x1 4.67 us: per_device(): value_rows = lax.all_gather(chosen_v[None], 'seq', axis=0, tiled=True)]
  transfers between devices with their start and end apart: 4 -> 0, of which waited for: 4 -> 0; matrix products, arithmetic and copies ran while one was open for 17% -> 0% of each run, Pallas kernels for 0% -> 0%
where the time goes in v1:
time: 89.6 us; the launch traced here: 89.5 us
  Pallas kernels  82.8 us (92%)
  local copies, waits for them, and re-layouts  3.89 us (4%)
  other arithmetic  2.09 us (2%)
    pallas_call x1, Pallas kernels, per_device(): pl.pallas_call(functools.partial(step_kernel, n_seq), out_shape=jax.Shape...  82.8 us
    unnamed x1, local copies, waits for them, and re-layouts  2.65 us

profile of v1, /device:TPU:0, one launch (start us, length us, event | category | flops | bytes accessed | tf_op | source)
XLA Modules:
  0.0 89.5 jit_solution(13269893623826976800)
XLA Ops:
  0.0 1.2 %dynamic_slice.4 = s32[1]{0:T(128)} dynamic-slice(s32[4]{0:T(128)} %param.25, s32[]{:T(128)S(6)} %select_n.44), dynamic_slice_sizes={1} | dynamic-slice | bytes 12 | tf_op jit(solution)/shard_map/jit(dynamic_index_in_dim)/dynamic_slice | solution.py:406
  1.9 0.5 fusion.2
  2.5 0.8 pad_maximum_fusion.1.sin_ref
  3.2 0.8 pad_maximum_fusion.cos_ref
  4.0 82.8 %joint_step.1 = bf16[2,256,1536]{2,1,0:T(8,128)(2,1)} custom-call(s32[4]{0:T(128)} %refresh_ref.1, s32[2]{0:T(128)} %len_ref.1, f32[3,2,3072]{2,1,0:T(2,128)} %bitcast.6, f32[1,128]{1,0:T(1,128)} %bitcast.7, f32[1,128]{1,0:T(1,128)} %bitcast.8, f32[256,128]{1,0:T(8,128)} %pad_maximum_fusion.cos_ref, f32[256,128]{1,0:T(8,128)} %pad_maximum_fusion.1.sin_ref, ...), custom_call_target="tpu_custom_call" | custom-call | tf_op jit(solution)/shard_map/joint_step/pallas_call | solution.py:417
  86.8 2.7 %copy.16 = bf16[2,256,1536]{2,1,0:T(8,128)(2,1)} copy(bf16[2,256,1536]{2,1,0:T(8,128)(2,1)} %joint_step.1) | data formatting | bytes 3145728
  (3 shorter events, 0.0 us)

commit v2 on v1

--- a/solution.py
+++ b/solution.py
@@ -8,7 +8,11 @@
 from jax.sharding import PartitionSpec as P
 
 GRID_W = 64
-CHUNKS = 2
+FIRST = (4, 4, 2)
+LAST = (2, 4, 4)
+MIDDLE = (2, 2)
+LAG = 2
+W_SPREAD = 0
 TILE = 512
 PAIR = 256
 
@@ -20,7 +24,8 @@
     half_dim = head_dim // 2
     first_pairs = head_dim // 16
     axis_pairs = (half_dim - first_pairs) // 2
-    pair_index = jnp.arange(half_dim, dtype=jnp.int32)
+    lane = jnp.arange(head_dim, dtype=jnp.int32)
+    pair_index = lane % half_dim
     pair_local = jnp.where(
         pair_index < first_pairs + axis_pairs,
         pair_index - first_pairs,
@@ -36,9 +41,18 @@
         pair_index[None, :] < first_pairs + axis_pairs, row_pos[:, None], col_pos[:, None]
     )
     angles = position * frequency[None, :]
-    cosine = jnp.cos(angles)
-    sine = jnp.sin(angles)
-    return (jnp.concatenate([cosine, cosine], axis=-1), jnp.concatenate([-sine, sine], axis=-1))
+    sign = jnp.where(lane < half_dim, -1.0, 1.0)
+    return jnp.cos(angles), jnp.sin(angles) * sign[None, :]
+
+
+def chunk_table(prompts, tok_rows):
+    table = []
+    for p in range(prompts):
+        r0 = 0
+        for cut in FIRST if p == 0 else LAST if p == prompts - 1 else MIDDLE:
+            table.append((p, r0, tok_rows // cut))
+            r0 += tok_rows // cut
+    return table
 
 
 def rms_rotate(vectors, gain, cos_rows, sin_rows):
@@ -49,6 +63,7 @@
 
 def step_kernel(
     n_seq,
+    n_batch,
     refresh_ref,
     len_ref,
     mod_ref,
@@ -67,16 +82,15 @@
     out_ref,
     xin,
     weights,
-    wout,
+    wfull,
     kv,
     chosen,
     queries,
     attended,
-    out_send,
-    out_recv,
+    partial,
     result,
     text,
-    scores,
+    score_slots,
     modulated,
     load_sem,
     store_sem,
@@ -89,18 +103,24 @@
     relay_send,
     part_send,
     part_recv,
+    w_send,
+    w_recv,
+    w_spread,
 ):
     prompts, tok_rows, width_part = image_ref.shape
     model_width = 2 * width_part
-    channels = wout.shape[0]
+    channels = wout_ref.shape[0]
     head_dim = cos_ref.shape[1]
     heads = channels // head_dim
     text_rows = tk_ref.shape[1]
     total_text = text_rows * n_seq
-    rows = tok_rows // CHUNKS
-    n_chunks = prompts * CHUNKS
+    table = chunk_table(prompts, tok_rows)
+    n_chunks = len(table)
     n_tiles = width_part // TILE
     n_chips = n_seq // 2
+    n_pairs = channels // PAIR
+    w_rows = channels // (2 * n_batch)
+    part = lax.axis_index("batch")
     me = lax.axis_index("seq")
     side = lax.axis_index("head")
     core = lax.rem(me, 2)
@@ -127,7 +147,11 @@
         pltpu.make_async_copy(sv_ref, chosen.at[1], load_sem.at[5]),
         pltpu.make_async_copy(tk_ref, text.at[0, :, pl.ds(me * text_rows, text_rows)], load_sem.at[6]),
         pltpu.make_async_copy(tv_ref, text.at[1, :, pl.ds(me * text_rows, text_rows)], load_sem.at[7]),
-        pltpu.make_async_copy(wout_ref, wout, load_sem.at[8]),
+        pltpu.make_async_copy(
+            wout_ref.at[:, pl.ds(pl.multiple_of(side * width_part, width_part), width_part)],
+            wfull.at[side],
+            load_sem.at[8],
+        ),
         pltpu.make_async_copy(cached_ref, result, load_sem.at[9]),
     ]
     for copy in loads:
@@ -138,10 +162,13 @@
         peer = lax.rem(me + d, n_seq)
         pl.semaphore_signal(barrier, inc=1, device_id={"seq": peer}, device_id_type=pl.DeviceIdType.MESH)
     pl.semaphore_signal(barrier, inc=1, device_id={"head": other}, device_id_type=pl.DeviceIdType.MESH)
-    pl.semaphore_wait(barrier, n_seq)
+    for d in range(1, n_batch):
+        peer = lax.rem(part + d, n_batch)
+        pl.semaphore_signal(barrier, inc=1, device_id={"batch": peer}, device_id_type=pl.DeviceIdType.MESH)
+    pl.semaphore_wait(barrier, n_seq + n_batch - 1)
 
     def image_copy(c, half):
-        p, r0 = c // CHUNKS, (c % CHUNKS) * rows
+        p, r0, rows = table[c]
         return remote(
             image_ref.at[p, pl.ds(r0, rows)],
             xin.at[half, p, pl.ds(r0, rows)],
@@ -160,7 +187,7 @@
         )
 
     def kv_copy(c, src, owner, send, where):
-        p, r0 = c // CHUNKS, (c % CHUNKS) * rows
+        p, r0, rows = table[c]
         return remote(
             src.at[:, p, pl.ds(r0, rows)],
             kv.at[owner, :, p, pl.ds(r0, rows)],
@@ -169,15 +196,61 @@
             where,
         )
 
-    def part_copy(p, t):
-        return remote(
-            out_send.at[p, t],
-            out_recv.at[p, t],
-            part_send.at[p, t],
-            part_recv.at[p, t],
+    def part_copy(p, j, half):
+        cols = pl.ds(j * PAIR if isinstance(j, int) else pl.multiple_of(j * PAIR, PAIR), PAIR)
+        return remote(
+            attended.at[half, p, :, cols],
+            attended.at[half, p, :, cols],
+            part_send.at[p, j],
+            part_recv.at[p, j],
             {"head": other},
         )
 
+    def w_block(owner, which):
+        return wfull.at[other, pl.ds((owner * 2 + which) * w_rows, w_rows)]
+
+    def w_cross(half):
+        block = pl.ds((part * 2 + core) * w_rows, w_rows)
+        cols = pl.ds(pl.multiple_of(other * width_part, width_part), width_part)
+        return remote(
+            wout_ref.at[block, cols],
+            wfull.at[half, block],
+            w_send.at[0],
+            w_recv.at[part, core],
+            {"head": other},
+        )
+
+    def w_along(owner, d, where):
+        return remote(
+            w_block(owner, core), w_block(owner, core), w_send.at[d], w_recv.at[owner, core], where
+        )
+
+    def w_to_sibling(owner, which, d):
+        return remote(
+            w_block(owner, which),
+            w_block(owner, which),
+            w_spread.at[d],
+            w_recv.at[owner, which],
+            {"seq": sibling},
+        )
+
+    def spread_weights():
+        w_cross(other).wait_recv()
+        for d in range(1, n_batch):
+            w_along(part, d, {"batch": lax.rem(part + d, n_batch)}).start()
+        w_to_sibling(part, core, 0).start()
+
+    def relay_weights():
+        for d in range(1, n_batch):
+            owner = lax.rem(part + n_batch - d, n_batch)
+            w_along(owner, d, {"batch": owner}).wait_recv()
+            w_to_sibling(owner, core, d).start()
+
+    def weights_here():
+        for d in range(n_batch):
+            w_to_sibling(lax.rem(part + d, n_batch), 1 - core, d).wait_recv()
+
+    w_cross(side).start()
     image_copy(0, side).start()
     image_copy(1, side).start()
     for d in range(1, n_seq):
@@ -187,7 +260,7 @@
     fresh_flag = refresh_ref[me] == 1
 
     def project(c):
-        p, r0 = c // CHUNKS, (c % CHUNKS) * rows
+        p, r0, rows = table[c]
         block = pl.ds(r0, rows)
         if c == 0:
             loads[0].wait()
@@ -209,7 +282,7 @@
         inverse = lax.rsqrt(variance + epsilon)
         for half, values in ((0, left), (1, right)):
             cols = pl.ds(half * width_part, width_part)
-            modulated[:, cols] = (
+            modulated[pl.ds(0, rows), cols] = (
                 values * inverse * (1.0 + mod_ref[1, pl.ds(p, 1), cols])
                 + mod_ref[0, pl.ds(p, 1), cols]
             ).astype(jnp.bfloat16)
@@ -222,7 +295,7 @@
         def pair(j, carry):
             start = pl.multiple_of(j * PAIR, PAIR)
             cols = pl.ds(start, PAIR)
-            x = modulated[...]
+            x = modulated[pl.ds(0, rows)]
 
             def rotated(index, gain):
                 raw = jnp.dot(x, weights[index, :, cols], preferred_element_type=jnp.float32)
@@ -280,7 +353,8 @@
                 total = op(total, values[:, i : i + 128])
             return total
 
-        def one_head(h, carry):
+        def one_head(h, slot):
+            scores = score_slots.at[slot]
             cols = pl.ds(pl.multiple_of(h * head_dim, head_dim), head_dim)
             q = queries[p, :, cols]
             s_text = times_transposed(q, text[0, p, :, cols])
@@ -310,18 +384,15 @@
 
             total, mixed = looped(n_seq, mix, (total, mixed))
             total = jnp.sum(total, axis=-1, keepdims=True)
-            attended[p, :, cols] = (mixed / total).astype(jnp.bfloat16)
+            attended[side, p, :, cols] = (mixed / total).astype(jnp.bfloat16)
+
+        def head_pair(j, carry):
+            for i in range(PAIR // head_dim):
+                one_head(j * (PAIR // head_dim) + i, i % score_slots.shape[0])
+            part_copy(p, j, side).start()
             return carry
 
-        lax.fori_loop(0, heads, one_head, 0)
-
-    def send_parts(p):
-        for t in range(n_tiles):
-            cols = pl.ds(pl.multiple_of(other * width_part + t * TILE, TILE), TILE)
-            out_send[p, t] = jnp.dot(
-                attended[p], wout[:, cols], preferred_element_type=jnp.float32
-            ).astype(jnp.bfloat16)
-            part_copy(p, t).start()
+        lax.fori_loop(0, n_pairs, head_pair, 0)
 
     def store(p, t):
         here = pl.ds(t * TILE, TILE)
@@ -330,47 +401,71 @@
         )
 
     def finish(p):
+        early = (n_pairs - 1) * PAIR
+
+        def accumulate(half, first, last, t):
+            return jnp.dot(
+                attended[half, p, :, first:last],
+                wfull[half, first:last, t * TILE : (t + 1) * TILE],
+                preferred_element_type=jnp.float32,
+            )
+
+        for t in range(n_tiles):
+            partial[t] = accumulate(side, 0, channels, t)
+        for j in range(n_pairs - 1):
+            part_copy(p, j, other).wait_recv()
+        for t in range(n_tiles):
+            partial[t] += accumulate(other, 0, early, t)
+        part_copy(p, n_pairs - 1, other).wait_recv()
         for t in range(n_tiles):
             cols = pl.ds(pl.multiple_of(side * width_part + t * TILE, TILE), TILE)
             here = pl.ds(t * TILE, TILE)
-            own = jnp.dot(attended[p], wout[:, cols], preferred_element_type=jnp.float32)
-            part_copy(p, t).wait_recv()
+            whole = partial[t] + accumulate(other, early, channels, t)
             gate = mod_ref[2, pl.ds(p, 1), cols]
             result[p, :, here] = (
                 xin[side, p, :, here].astype(jnp.float32)
-                + gate * (own + out_recv[p, t].astype(jnp.float32))
+                + gate * whole
                 + result[p, :, here].astype(jnp.float32)
             ).astype(jnp.bfloat16)
             store(p, t).start()
 
-    project(0)
-    for c in range(1, n_chunks):
+    def attend_all(p):
+        for k in range(n_chunks):
+            if table[k][0] == p:
+                arrive(k)
+        attend(p)
+
+    for c in range(n_chunks):
         project(c)
-        relay(c - 1)
-        if c == CHUNKS:
-            for copy in loads[6:]:
-                copy.wait()
-            for d in range(1, n_seq):
-                for i in range(2):
-                    text_copy(i, lax.rem(me + d, n_seq), d, {"seq": sibling}).wait_recv()
-        if c >= CHUNKS and c % CHUNKS == 0:
-            p = c // CHUNKS - 1
-            for k in range(p * CHUNKS, (p + 1) * CHUNKS):
-                arrive(k)
-            attend(p)
-            send_parts(p)
-    relay(n_chunks - 1)
-    for k in range(n_chunks - CHUNKS, n_chunks):
-        arrive(k)
-    attend(prompts - 1)
-    send_parts(prompts - 1)
+        if c == W_SPREAD:
+            spread_weights()
+        if c >= LAG:
+            relay(c - LAG)
+    for copy in loads[6:]:
+        copy.wait()
+    for d in range(1, n_seq):
+        for i in range(2):
+            text_copy(i, lax.rem(me + d, n_seq), d, {"seq": sibling}).wait_recv()
+    for p in range(prompts - 1):
+        attend_all(p)
+    for c in range(n_chunks - LAG, n_chunks):
+        relay(c)
+    attend_all(prompts - 1)
+    relay_weights()
+    weights_here()
     for p in range(prompts):
         finish(p)
 
     for p in range(prompts):
+        for j in range(n_pairs):
+            part_copy(p, j, side).wait_send()
         for t in range(n_tiles):
-            part_copy(p, t).wait_send()
             store(p, t).wait()
+    w_cross(side).wait_send()
+    for d in range(1, n_batch):
+        w_along(part, d, {"batch": lax.rem(part + d, n_batch)}).wait_send()
+    for d in range(n_batch):
+        w_to_sibling(lax.rem(part + n_batch - d, n_batch), core, d).wait_send()
     for c in range(n_chunks):
         for d in range(n_chips):
             kv_copy(c, chosen, me, kv_send.at[d, c], {"seq": sibling}).wait_send()
@@ -383,6 +478,7 @@
 
 def per_device(
     n_seq,
+    n_batch,
     image_hidden,
     modulation,
     qkv_weight,
@@ -403,10 +499,11 @@
     channels, model_width = out_weight.shape
     text_rows = text_keys.shape[1]
     seq_seat = lax.axis_index("seq")
-    own_band = lax.dynamic_index_in_dim(patch_of, seq_seat, 0, keepdims=False)
+    seats = jnp.arange(n_seq, dtype=jnp.int32)
+    own_band = jnp.sum(jnp.where(seats == seq_seat, patch_of, 0))
     raster = own_band * tok_rows + jnp.arange(tok_rows, dtype=jnp.int32)
     cos_full, sin_full = rotary_tables(raster, head_dim, GRID_W)
-    n_chunks = prompts * CHUNKS
+    n_chunks = len(chunk_table(prompts, tok_rows))
     n_tiles = width_part // TILE
     n_chips = n_seq // 2
     bf16 = jnp.bfloat16
@@ -415,24 +512,23 @@
     vmem = pl.BlockSpec(memory_space=pltpu.VMEM)
     anywhere = pl.BlockSpec(memory_space=pl.ANY)
     return pl.pallas_call(
-        functools.partial(step_kernel, n_seq),
+        functools.partial(step_kernel, n_seq, n_batch),
         out_shape=jax.ShapeDtypeStruct(image_hidden.shape, bf16),
         in_specs=[smem] * 2 + [vmem] * 5 + [anywhere] * 8,
         out_specs=anywhere,
         scratch_shapes=[
             pltpu.VMEM((2, prompts, tok_rows, width_part), bf16),
             pltpu.VMEM((3, model_width, channels), bf16),
-            pltpu.VMEM((channels, model_width), bf16),
+            pltpu.VMEM((2, channels, width_part), bf16),
             pltpu.VMEM((n_seq, 2, prompts, tok_rows, channels), bf16),
             pltpu.VMEM((2, prompts, tok_rows, channels), bf16),
             pltpu.VMEM((prompts, tok_rows, channels), bf16),
-            pltpu.VMEM((prompts, tok_rows, channels), bf16),
-            pltpu.VMEM((prompts, n_tiles, tok_rows, TILE), bf16),
-            pltpu.VMEM((prompts, n_tiles, tok_rows, TILE), bf16),
+            pltpu.VMEM((2, prompts, tok_rows, channels), bf16),
+            pltpu.VMEM((n_tiles, tok_rows, TILE), jnp.float32),
             pltpu.VMEM((prompts, tok_rows, width_part), bf16),
             pltpu.VMEM((2, prompts, text_rows * n_seq, channels), bf16),
-            pltpu.VMEM((n_seq, tok_rows, tok_rows), jnp.float32),
-            pltpu.VMEM((tok_rows // CHUNKS, model_width), bf16),
+            pltpu.VMEM((2 if n_seq <= 4 else 1, n_seq, tok_rows, tok_rows), jnp.float32),
+            pltpu.VMEM((tok_rows // 2, model_width), bf16),
             dma((10,)),
             dma((prompts, n_tiles)),
             dma((n_chunks,)),
@@ -442,8 +538,11 @@
             dma((n_chips, n_chunks)),
             dma((n_seq, n_chunks)),
             dma((n_chips, n_chunks)),
-            dma((prompts, n_tiles)),
-            dma((prompts, n_tiles)),
+            dma((prompts, channels // PAIR)),
+            dma((prompts, channels // PAIR)),
+            dma((n_batch,)),
+            dma((n_batch, 2)),
+            dma((n_batch,)),
         ],
         compiler_params=pltpu.CompilerParams(
             collective_id=0, has_side_effects=True, vmem_limit_bytes=67043328
@@ -487,7 +586,7 @@
     )
     out_specs = P("batch", "seq", "head")
     return jax.shard_map(
-        functools.partial(per_device, mesh.shape["seq"]),
+        functools.partial(per_device, mesh.shape["seq"], mesh.shape["batch"]),
         mesh=mesh,
         in_specs=in_specs,
         out_specs=out_specs,

time: 89.6 us -> 81.1 us (0.905)
  Pallas kernels: 82.8 us -> 75 us
  local copies, waits for them, and re-layouts: 3.89 us -> 2.65 us
    pallas_call x1, Pallas kernels: 82.8 us -> 75 us  [per_device(): pl.pallas_call(functools.partial(step_kernel, n_seq, n_batch), out_shape=...]
    concatenate x2 -> x0, other arithmetic: 1.52 us -> none  [the longest x1 0.76 us: rotary_tables(): jnp.concatenate([cosine, cosine], axis=-1)]
    reduce_sum x0 -> x1, other arithmetic: none -> 1.29 us  [per_device(): own_band = jnp.sum(jnp.where(seats == seq_seat, patch_of, 0))]
    mul x0 -> x1, other arithmetic: none -> 1.26 us  [rotary_tables(): return (jnp.cos(angles), jnp.sin(angles) * sign[None, :])]
    dynamic_slice x1 -> x0, local copies, waits for them, and re-layouts: 1.24 us -> none  [per_device(): own_band = lax.dynamic_index_in_dim(patch_of, seq_seat, 0, keepdims=False)]
where the time goes in v2:
time: 81.1 us; the launch traced here: 80.9 us
  Pallas kernels  75 us (92%)
  local copies, waits for them, and re-layouts  2.65 us (3%)
  other arithmetic  2.58 us (3%)
    pallas_call x1, Pallas kernels, per_device(): pl.pallas_call(functools.partial(step_kernel, n_seq, n_batch), out_shape=...  75 us
    unnamed x1, local copies, waits for them, and re-layouts  2.65 us

profile of v2, /device:TPU:0, one launch (start us, length us, event | category | flops | bytes accessed | tf_op | source)
XLA Modules:
  0.0 80.9 jit_solution(2495921244728424629)
XLA Ops:
  0.0 1.3 %fusion.4 = s32[]{:T(128)} fusion(s32[4]{0:T(128)} %param.25, s32[]{:T(128)S(6)} %axis_index.15), kind=kLoop, calls=%fused_computation.16 | loop fusion | flops 11 | bytes 24 | tf_op jit(solution)/shard_map/reduce_sum | solution.py:503
  2.0 1.3 %sine_multiply_fusion = (f32[256,128]{1,0:T(8,128)}, f32[256,128]{1,0:T(8,128)}) fusion(f32[128]{0:T(128)S(1)} %get-tuple-element.9, f32[128]{0:T(128)S(1)} %get-tuple-element.10, f32[256]{0:T(256)S(1)} %get-tuple-element.7, f32[256]{0:T(256)S(1)} %get-tuple-element.8, pred[128]{0:T(512)(128)(4,1)S(1)} %broadcast_compare_fusion.1), kind=kLoop, calls=%fused_computation | loop fusion | flops 98304 | bytes 265344 | tf_op jit(solution)/shard_map/mul | solution.py:45
  3.3 75.0 %joint_step.1 = bf16[2,256,1536]{2,1,0:T(8,128)(2,1)} custom-call(s32[4]{0:T(128)} %refresh_ref.1, s32[2]{0:T(128)} %len_ref.1, f32[3,2,3072]{2,1,0:T(2,128)} %bitcast.5, f32[1,128]{1,0:T(1,128)} %bitcast.6, f32[1,128]{1,0:T(1,128)} %bitcast.7, f32[256,128]{1,0:T(8,128)} %get-tuple-element.6.cos_ref, f32[256,128]{1,0:T(8,128)} %get-tuple-element.5.sin_ref, ...), custom_call_target="tpu_custom_call" | custom-call | tf_op jit(solution)/shard_map/joint_step/pallas_call | solution.py:514
  78.2 2.7 %copy.16 = bf16[2,256,1536]{2,1,0:T(8,128)(2,1)} copy(bf16[2,256,1536]{2,1,0:T(8,128)(2,1)} %joint_step.1) | data formatting | bytes 3145728
  (3 shorter events, 0.0 us)
